TPU v7x, 32 devices: a whole 2x2x4 slice. The times are simulated.
32 devices in a mesh: grp: 4 (over x, core), gx: 2 (over y), gy: 4 (over z).
Axes of the slice: x: 2, y: 2, z: 4, core: 2. Of those that a mesh axis runs over, the one named last changes fastest.
Arguments:
- pressure: float32 [24, 128, 1024], P(None, ('grp', 'gy'), 'gx'), may hold values from -2 to 0.2
- soil_class: int32 [24, 128, 1024], P(None, ('grp', 'gy'), 'gx'), may hold values from 0 to 11
- capacity_range: float32 [12], replicated, may hold values from 0.25 to 0.45
- inverse_entry: float32 [12], replicated, may hold values from 0.3 to 3
- shape_index: float32 [12], replicated, may hold values from 1.3 to 2.5
- conductivity: float32 [12], replicated, may hold values from 0.05 to 1
- depth: float32 [128, 1024], P('grp', ('gx', 'gy')), may hold values from 0 to 2
- elevation: float32 [128, 1024], P('grp', ('gx', 'gy')), may hold values from -4 to 4
- roughness: float32 [128, 1024], P('grp', ('gx', 'gy')), may hold values from 2 to 8
- rain: float32 [128, 1024], P('grp', ('gx', 'gy')), may hold values from 0.1 to 1
- land_mask: int32 [128, 1024], P('grp', ('gx', 'gy')), may hold values 0 or 1
- channel_mask: int32 [128, 1024], P('grp', ('gx', 'gy')), may hold values 0 or 1
Outputs:
- head: float32 [24, 128, 1024], P(None, ('grp', 'gy'), 'gx')
- water: float32 [128, 1024], P('grp', ('gx', 'gy'))
All inputs are finite; a program needn't handle non-finite values. No bound on the sum of `land_mask` or of `channel_mask` on one device may be relied on, other than what follows from the above.
Results may differ from a plain program's by a relative error of at most 0.0003.
Values sent between devices are 32-bit elements; how exact they have to be, the bound alone decides.
No kernel may reach another device: no remote copies, remote signals or barrier semaphores. Data moves between devices by JAX's collectives and lax.ppermute only.
A program may use at most 64 MiB of HBM per device.

v0:
```python
import jax
import jax.numpy as jnp
from jax import lax
from jax.sharding import PartitionSpec as P

SWEEPS = 2
PASSES = 3
STORAGE = 0.01
LATERAL = 4.0
VERTICAL = 4.0
GRAVITY_STEP = 0.5
SUCTION_FLOOR = 0.01
SLOPE_FLOOR = 0.1
SURFACE_STEP = 0.3
LEAKANCE = 0.5
SOURCE_GAIN = 1.0


def with_halo(shard, sides, width):
    for axis, dim in sides:
        size, length = (lax.axis_size(axis), shard.shape[dim])
        up = [(i, (i + 1) % size) for i in range(size - 1)]
        down = [(j, i) for i, j in up]
        last = lax.slice_in_dim(shard, length - width, length, axis=dim)
        leading = lax.slice_in_dim(shard, 0, width, axis=dim)
        before = lax.ppermute(last, axis, up)
        after = lax.ppermute(leading, axis, down)
        shard = jnp.concatenate([before, shard, after], axis=dim)
    return shard


def lookup(soil_class, tables):
    results = []
    for table in tables:
        filled = jnp.zeros(soil_class.shape, table.dtype)
        for kind_number in range(table.shape[0]):
            filled = jnp.where(soil_class == kind_number, table[kind_number], filled)
        results.append(filled)
    return results


def closures(pressure, capacity_range, inverse_entry, pore_index, conductivity):
    exponent = 1.0 / (1.0 - pore_index)
    scaled = jnp.maximum(-inverse_entry * pressure, SUCTION_FLOOR)
    log_scaled = jnp.log(scaled)
    log_sum = jnp.log1p(jnp.exp(exponent * log_scaled))
    saturation = jnp.exp(-pore_index * log_sum)
    content = capacity_range * saturation
    capacity = STORAGE + capacity_range * pore_index * exponent * inverse_entry * jnp.exp(
        (exponent - 1.0) * log_scaled - (pore_index + 1.0) * log_sum
    )
    conduct = (
        conductivity
        * jnp.sqrt(saturation)
        * jnp.square(1.0 - jnp.exp(pore_index * (exponent * log_scaled - log_sum)))
    )
    return (content, capacity, conduct)


def update_cells(padded, conduct_pad, capacity, content_gap, source):
    layers = padded.shape[0] - 2
    rows = padded.shape[1] - 2
    cols = padded.shape[2] - 2
    center = padded[1:-1, 1:-1, 1:-1]
    own_conduct = conduct_pad[1:-1, 1:-1, 1:-1]
    numerator = capacity * center - content_gap
    denominator = capacity
    neighbours = (
        (1, 0, 1, LATERAL, 0.0),
        (1, 2, 1, LATERAL, 0.0),
        (1, 1, 0, LATERAL, 0.0),
        (1, 1, 2, LATERAL, 0.0),
        (0, 1, 1, VERTICAL, GRAVITY_STEP),
        (2, 1, 1, VERTICAL, -GRAVITY_STEP),
    )
    for first, second, third, weight, offset in neighbours:
        beside = padded[first : first + layers, second : second + rows, third : third + cols]
        beside_conduct = conduct_pad[
            first : first + layers, second : second + rows, third : third + cols
        ]
        face_weight = weight * jnp.sqrt(own_conduct * beside_conduct)
        numerator = numerator + face_weight * (beside + offset)
        denominator = denominator + face_weight
    gained = jnp.concatenate(
        [(SOURCE_GAIN * source)[None], jnp.zeros((layers - 1, rows, cols), source.dtype)], axis=0
    )
    numerator = numerator + gained
    return numerator / denominator


def face_flux(upper_level, lower_level, upper_depth, lower_depth, upper_convey, lower_convey):
    slope = upper_level - lower_level
    upwind = jnp.where(slope >= 0, upper_depth, lower_depth)
    carried = upwind * jnp.cbrt(upwind * upwind)
    return (
        jnp.sqrt(upper_convey * lower_convey)
        * carried
        * slope
        / jnp.sqrt(jnp.maximum(jnp.abs(slope), SLOPE_FLOOR))
    )


def overland(depth_pad, level_pad, convey_pad, leak, top, rain):
    current = depth_pad[1:-1, 1:-1]
    surface = level_pad + depth_pad
    across = face_flux(
        surface[:-1, 1:-1],
        surface[1:, 1:-1],
        depth_pad[:-1, 1:-1],
        depth_pad[1:, 1:-1],
        convey_pad[:-1, 1:-1],
        convey_pad[1:, 1:-1],
    )
    along = face_flux(
        surface[1:-1, :-1],
        surface[1:-1, 1:],
        depth_pad[1:-1, :-1],
        depth_pad[1:-1, 1:],
        convey_pad[1:-1, :-1],
        convey_pad[1:-1, 1:],
    )
    outflow = across[1:] - across[:-1] + (along[:, 1:] - along[:, :-1])
    rate = leak * (current - top)
    return (jnp.maximum(current + SURFACE_STEP * (rain - rate - outflow), 0.0), rate)


def trim_edges(field, margin):
    rows = field.shape[-2]
    cols = field.shape[-1]
    return field[..., margin : rows - margin, margin : cols - margin]


def pad_layers(field):
    return jnp.pad(field, ((1, 1), (0, 0), (0, 0)))


def local(
    pressure,
    soil_class,
    capacity_range,
    inverse_entry,
    shape_index,
    conductivity,
    depth,
    elevation,
    roughness,
    rain,
    land_mask,
    channel_mask,
):
    pore_table = 1.0 - 1.0 / shape_index
    tables = (capacity_range, inverse_entry, pore_table, conductivity)
    range_cells, entry_cells, pore_cells, conduct_cells = lookup(soil_class, tables)
    content0, capacity, conduct = closures(
        pressure, range_cells, entry_cells, pore_cells, conduct_cells
    )
    top_conduct = conduct[0]
    top, top_surface = (
        lax.all_to_all(pressure[0], "gy", split_axis=1, concat_axis=0, tiled=True),
        lax.all_to_all(top_conduct, "gy", split_axis=1, concat_axis=0, tiled=True),
    )
    leak = LEAKANCE * land_mask.astype(jnp.float32) * top_surface
    convey = (1.0 + channel_mask.astype(jnp.float32)) / roughness
    exchange = jnp.zeros_like(depth)
    surface_pad = with_halo(
        jnp.stack([depth, elevation, convey, leak, top, rain]),
        (("grp", 1), (("gx", "gy"), 2)),
        PASSES,
    )
    water = surface_pad[0]
    for pass_number in range(PASSES):
        water, rate = overland(
            water,
            trim_edges(surface_pad[1], pass_number),
            trim_edges(surface_pad[2], pass_number),
            trim_edges(surface_pad[3], pass_number + 1),
            trim_edges(surface_pad[4], pass_number + 1),
            trim_edges(surface_pad[5], pass_number + 1),
        )
        exchange = exchange + SURFACE_STEP * trim_edges(rate, PASSES - pass_number - 1)
    source = lax.all_to_all(exchange, "gy", split_axis=0, concat_axis=1, tiled=True)
    head = pressure
    content = content0
    for sweep_number in range(SWEEPS):
        soil_rim = with_halo(jnp.stack([head, conduct]), ((("grp", "gy"), 2), ("gx", 3)), 1)
        head = update_cells(
            pad_layers(soil_rim[0]), pad_layers(soil_rim[1]), capacity, content - content0, source
        )
        if sweep_number + 1 < SWEEPS:
            content, capacity, conduct = closures(
                head, range_cells, entry_cells, pore_cells, conduct_cells
            )
    return (head, water)


def solution(mesh):
    return jax.shard_map(
        local,
        mesh=mesh,
        in_specs=(
            P(None, ("grp", "gy"), "gx"),
            P(None, ("grp", "gy"), "gx"),
            P(),
            P(),
            P(),
            P(),
            P("grp", ("gx", "gy")),
            P("grp", ("gx", "gy")),
            P("grp", ("gx", "gy")),
            P("grp", ("gx", "gy")),
            P("grp", ("gx", "gy")),
            P("grp", ("gx", "gy")),
        ),
        out_specs=(P(None, ("grp", "gy"), "gx"), P("grp", ("gx", "gy"))),
        check_vma=False,
    )
```

profile of v0, /device:TPU:1, one launch (start us, length us, event | category | flops | bytes accessed | tf_op | source)
XLA Modules:
  0.0 136.5 jit_solution(11352913227923329193)
XLA Ops:
  0.7 1.8 %fusion.114 = (f32[1]{0:T(128)}, f32[1]{0:T(128)}, f32[1]{0:T(128)}, f32[1]{0:T(128)}, f32[1]{0:T(128)}, /*index=5*/f32[1]{0:T(128)}, f32[1]{0:T(128)}, f32[1]{0...) fusion(f32[12]{0:T(128)} %param.15), kind=kLoop, calls=%fused_computation.231 | loop fusion | bytes 96 | tf_op jit(solution)/shard_map/slice | solution.py:37
  2.5 1.8 %fusion.113 = (f32[1]{0:T(128)}, f32[1]{0:T(128)}, f32[1]{0:T(128)}, f32[1]{0:T(128)}, f32[1]{0:T(128)}, /*index=5*/f32[1]{0:T(128)}, f32[1]{0:T(128)}, f32[1]{0...) fusion(f32[12]{0:T(128)} %param.17), kind=kLoop, calls=%fused_computation.230 | loop fusion | bytes 96 | tf_op jit(solution)/shard_map/slice | solution.py:37
  4.3 0.7 divide_subtract_fusion
  4.9 0.7 fusion.112
  5.6 26.2 %multiply_multiply_fusion = (f32[24,8,512]{2,1,0:T(8,128)S(1)}, f32[24,8,512]{2,1,0:T(8,128)S(1)}, f32[24,8,512]{2,1,0:T(8,128)S(1)}, f32[24,8,512]{2,1,0:T(8,12...) fusion(f32[24,8,512]{2,1,0:T(8,128)} %param.12, ...), kind=kLoop, calls=%fused_computation.100 | loop fusion | flops 6094848 | bytes 3539088 | tf_op jit(solution)/shard_map/mul | solution.py:53
  31.9 0.6 slice_bitcast_fusion.10
  32.5 5.4 %all-to-all-start = ((f32[8,4,128]{2,0,1:T(8,128)}), f32[8,4,128]{2,0,1:T(8,128)S(1)}, u32[]{:S(2)}, u32[]{:S(2)}) async-start(f32[8,4,128]{2,0,1:T(8,128)} %slice_bitcast_fusion.10), calls=%async_computation | async-start | bytes 32768 | tf_op jit(solution)/shard_map/all_to_all | solution.py:160
  38.0 0.6 slice_bitcast_fusion.11
  38.6 3.8 %all-to-all-done = f32[8,4,128]{2,0,1:T(8,128)S(1)} async-done(((f32[8,4,128]{2,0,1:T(8,128)}), f32[8,4,128]{2,0,1:T(8,128)S(1)}, u32[]{:S(2)}, u32[]{:S(2)}) %all-to-all-start) | async-done | bytes 16416 | tf_op jit(solution)/shard_map/all_to_all | solution.py:160
  42.3 3.2 %all-to-all-start.1 = ((f32[8,4,128]{2,0,1:T(8,128)}), f32[8,4,128]{2,0,1:T(8,128)S(1)}, u32[]{:S(2)}, u32[]{:S(2)}) async-start(f32[8,4,128]{2,0,1:T(8,128)} %slice_bitcast_fusion.11), calls=%async_computation.1 | async-start | bytes 32768 | tf_op jit(solution)/shard_map/all_to_all | solution.py:159
  45.6 4.4 %all-to-all-done.1 = f32[8,4,128]{2,0,1:T(8,128)S(1)} async-done(((f32[8,4,128]{2,0,1:T(8,128)}), f32[8,4,128]{2,0,1:T(8,128)S(1)}, u32[]{:S(2)}, u32[]{:S(2)}) %all-to-all-start.1) | async-done | bytes 16416 | tf_op jit(solution)/shard_map/all_to_all | solution.py:159
  50.1 5.2 %collective-permute-start.5 = (f32[6,3,128]{2,1,0:T(4,128)S(1)}, f32[6,3,128]{2,1,0:T(4,128)S(1)}, u32[]{:S(2)}, u32[]{:S(2)}) collective-permute-start(f32[6,3,128]{2,1,0:T(4,128)S(1)} %get-tuple-element.50), channel_id=1, source_target_pairs={{8,0},{16,8},{24,16},{9,1},{17,9},{25,17},{10,2},{18,10},{26,18},{... | collective-permute-start | bytes 27656 | tf_op jit(solution)/shard_map/ppermute | solution.py:27
  55.2 3.0 %collective-permute-start.4 = (f32[6,3,128]{2,1,0:T(4,128)S(1)}, f32[6,3,128]{2,1,0:T(4,128)S(1)}, u32[]{:S(2)}, u32[]{:S(2)}) collective-permute-start(f32[6,3,128]{2,1,0:T(4,128)S(1)} %get-tuple-element.49), channel_id=1, source_target_pairs={{0,8},{8,16},{16,24},{1,9},{9,17},{17,25},{2,10},{10,18},{18,26},{... | collective-permute-start | bytes 27656 | tf_op jit(solution)/shard_map/ppermute | solution.py:26
  58.4 1.9 %collective-permute-start.1 = (f32[2,24,1,512]{3,2,1,0:T(1,128)S(1)}, f32[2,24,1,512]{3,2,1,0:T(1,128)S(1)}, u32[]{:S(2)}, u32[]{:S(2)}) collective-permute-start(f32[2,24,1,512]{3,2,1,0:T(1,128)S(1)} %get-tuple-element.38), channel_id=1, source_target_pairs={{1,0},{2,1},{3,2},{8,3},{9,8},{10,9},{11,10},{16,11},{17,16},{18,1... | collective-permute-start | bytes 294920 | tf_op jit(solution)/shard_map/ppermute | solution.py:27
  60.3 3.4 %collective-permute-start = (f32[2,24,1,512]{3,2,1,0:T(1,128)S(1)}, f32[2,24,1,512]{3,2,1,0:T(1,128)S(1)}, u32[]{:S(2)}, u32[]{:S(2)}) collective-permute-start(f32[2,24,1,512]{3,2,1,0:T(1,128)S(1)} %get-tuple-element.37), channel_id=1, source_target_pairs={{0,1},{1,2},{2,3},{3,8},{8,9},{9,10},{10,11},{11,16},{16,17},{17,1... | collective-permute-start | bytes 294920 | tf_op jit(solution)/shard_map/ppermute | solution.py:26
  63.8 1.3 collective-permute-start.7
  65.1 4.0 %collective-permute-start.6 = (f32[6,38,3]{2,1,0:T(8,128)S(1)}, f32[6,38,3]{2,1,0:T(8,128)S(1)}, u32[]{:S(2)}, u32[]{:S(2)}) collective-permute-start(f32[6,38,3]{2,1,0:T(8,128)S(1)} %get-tuple-element.47), channel_id=1, source_target_pairs={{0,1},{1,2},{2,3},{3,4},{4,5},{5,6},{6,7},{8,9},{9,10},{10,11},{11... | collective-permute-start | bytes 8216 | tf_op jit(solution)/shard_map/ppermute | solution.py:26
  69.1 0.7 fusion.111
  69.8 2.2 %collective-permute-done.7 = f32[6,38,3]{2,1,0:T(8,128)S(1)} collective-permute-done((f32[6,38,3]{2,1,0:T(8,128)S(1)}, f32[6,38,3]{2,1,0:T(8,128)S(1)}, u32[]{:S(2)}, u32[]{:S(2)}) %collective-permute-start.7) | collective-permute-done | bytes 2768 | tf_op jit(solution)/shard_map/ppermute | solution.py:27
  72.0 0.2 pad_maximum_fusion.10
  72.2 0.1 fusion.78
  72.4 0.2 fusion.82
  72.5 0.1 slice_add_fusion.1
  72.7 0.1 fusion.64
  72.8 0.2 fusion.68
  73.0 0.1 slice_add_fusion
  73.4 0.3 pad_maximum_fusion.9
  73.7 0.3 copy-done.1
  74.1 1.3 collective-permute-start.3
  75.4 9.5 %collective-permute-start.2 = (f32[2,24,10,1]{3,2,1,0:T(8,128)S(1)}, f32[2,24,10,1]{3,2,1,0:T(8,128)S(1)}, u32[]{:S(2)}, u32[]{:S(2)}) collective-permute-start(f32[2,24,10,1]{3,2,1,0:T(8,128)S(1)} %get-tuple-element.33), channel_id=1, source_target_pairs={{0,4},{1,5},{2,6},{3,7},{8,12},{9,13},{10,14},{11,15},{16,20},{17,... | collective-permute-start | bytes 5768 | tf_op jit(solution)/shard_map/ppermute | solution.py:26
  84.8 0.7 fusion.96
  85.5 3.2 %all-to-all-start.2 = ((f32[4,8,128]{2,1,0:T(8,128)}), f32[4,8,128]{2,1,0:T(8,128)S(1)}, u32[]{:S(2)}, u32[]{:S(2)}) async-start(f32[4,8,128]{2,1,0:T(8,128)} %get-tuple-element.46), calls=%async_computation.2 | async-start | bytes 32768 | tf_op jit(solution)/shard_map/all_to_all | solution.py:181
  88.8 3.2 %collective-permute-done.3 = f32[2,24,10,1]{3,2,1,0:T(8,128)S(1)} collective-permute-done((f32[2,24,10,1]{3,2,1,0:T(8,128)S(1)}, f32[2,24,10,1]{3,2,1,0:T(8,128)S(1)}, u32[]{:S(2)}, u32[]{:S(2)}) %collective-permute-start.3) | collective-permute-done | bytes 1952 | tf_op jit(solution)/shard_map/ppermute | solution.py:27
  92.0 0.9 collective-permute-done.2
  92.9 2.4 %pad_maximum_fusion = f32[2,24,10,514]{3,2,1,0:T(8,128)S(1)} fusion(f32[2,24,10,1]{3,2,1,0:T(8,128)S(1)} %collective-permute-done.3, f32[2,24,1,512]{3,2,1,0:T(1,128)} %copy-done.1, f32[1,24,8,512]{3,2,1,0:T(8,128)S(1)} %bitcast.118, f32[1,24,8,512]{3,2,1,0:T(8,128)S(1)} %bitcast.112, f32[2,24,1,512]{3,2,1,0:T(1,128)} %copy-done.2, ...), kind=kLoop, calls=%fused_computation | loop fusion | flops 1233600 | bytes 1973760 | tf_op jit(solution)/shard_map/concatenate | solution.py:28
  95.3 0.1 slice_bitcast_fusion.2
  95.4 11.8 %multiply_bitcast_fusion = (f32[1,24,8,512]{3,2,1,0:T(8,128)S(1)}, f32[24,8,512]{2,1,0:T(8,128)S(1)}, f32[24,8,512]{2,1,0:T(8,128)S(1)}) fusion(f32[24,8,512]{2,1,0:T(8,128)S(1)} %get-tuple-element.14, f32[24,8,512]{2,1,0:T(8,128)S(1)} %get-tuple-element.13, f32[24,8,512]{2,1,0:T(8,128)S(1)} %get-tuple-element.12, f32[1,8,512]{2,1,0:T(8,128)S(1)} %bitcast.119, ...), kind=kLoop, calls=%fused_computation.94 | loop fusion | flops 7667712 | bytes 9846832 | tf_op jit(solution)/shard_map/stack | solution.py:185
  107.4 3.4 %collective-permute-start.9 = (f32[2,24,1,512]{3,2,1,0:T(1,128)S(1)}, f32[2,24,1,512]{3,2,1,0:T(1,128)S(1)}, u32[]{:S(2)}, u32[]{:S(2)}) collective-permute-start(f32[2,24,1,512]{3,2,1,0:T(1,128)S(1)} %get-tuple-element.36), channel_id=1, source_target_pairs={{1,0},{2,1},{3,2},{8,3},{9,8},{10,9},{11,10},{16,11},{17,16},{18,1... | collective-permute-start | bytes 294920 | tf_op jit(solution)/shard_map/ppermute | solution.py:27
  110.8 1.9 %collective-permute-start.8 = (f32[2,24,1,512]{3,2,1,0:T(1,128)S(1)}, f32[2,24,1,512]{3,2,1,0:T(1,128)S(1)}, u32[]{:S(2)}, u32[]{:S(2)}) collective-permute-start(f32[2,24,1,512]{3,2,1,0:T(1,128)S(1)} %get-tuple-element.35), channel_id=1, source_target_pairs={{0,1},{1,2},{2,3},{3,8},{8,9},{9,10},{10,11},{11,16},{16,17},{17,1... | collective-permute-start | bytes 294920 | tf_op jit(solution)/shard_map/ppermute | solution.py:26
  112.7 6.4 %collective-permute-done.8 = f32[2,24,1,512]{3,2,1,0:T(1,128)S(1)} collective-permute-done((f32[2,24,1,512]{3,2,1,0:T(1,128)S(1)}, f32[2,24,1,512]{3,2,1,0:T(1,128)S(1)}, u32[]{:S(2)}, u32[]{:S(2)}) %collective-permute-start.8) | collective-permute-done | bytes 98336 | tf_op jit(solution)/shard_map/ppermute | solution.py:26
  119.1 0.3 pad_maximum_fusion.5
  119.4 1.3 collective-permute-start.11
  120.7 4.3 %collective-permute-start.10 = (f32[2,24,10,1]{3,2,1,0:T(8,128)S(1)}, f32[2,24,10,1]{3,2,1,0:T(8,128)S(1)}, u32[]{:S(2)}, u32[]{:S(2)}) collective-permute-start(f32[2,24,10,1]{3,2,1,0:T(8,128)S(1)} %get-tuple-element.31), channel_id=1, source_target_pairs={{0,4},{1,5},{2,6},{3,7},{8,12},{9,13},{10,14},{11,15},{16,20},{17,... | collective-permute-start | bytes 5768 | tf_op jit(solution)/shard_map/ppermute | solution.py:26
  125.1 5.0 %collective-permute-done.11 = f32[2,24,10,1]{3,2,1,0:T(8,128)S(1)} collective-permute-done((f32[2,24,10,1]{3,2,1,0:T(8,128)S(1)}, f32[2,24,10,1]{3,2,1,0:T(8,128)S(1)}, u32[]{:S(2)}, u32[]{:S(2)}) %collective-permute-start.11) | collective-permute-done | bytes 1952 | tf_op jit(solution)/shard_map/ppermute | solution.py:27
  130.1 1.8 %collective-permute-done.10 = f32[2,24,10,1]{3,2,1,0:T(8,128)S(1)} collective-permute-done((f32[2,24,10,1]{3,2,1,0:T(8,128)S(1)}, f32[2,24,10,1]{3,2,1,0:T(8,128)S(1)}, u32[]{:S(2)}, u32[]{:S(2)}) %collective-permute-start.10) | collective-permute-done | bytes 1952 | tf_op jit(solution)/shard_map/ppermute | solution.py:26
  131.8 1.4 %pad_maximum_fusion.1 = f32[2,24,10,514]{3,2,1,0:T(8,128)S(1)} fusion(f32[2,24,10,1]{3,2,1,0:T(8,128)S(1)} %collective-permute-done.11, f32[2,24,1,512]{3,2,1,0:T(1,128)S(1)} %collective-permute-done.9, f32[1,24,8,512]{3,2,1,0:T(8,128)S(1)} %get-tuple-element.5, f32[1,24,8,512]{3,2,1,0:T(8,128)S(1)} %bitcast.115, ...), kind=kLoop, calls=%fused_computation.1 | loop fusion | flops 1233600 | bytes 1973760 | tf_op jit(solution)/shard_map/concatenate | solution.py:28
  133.3 0.1 slice_bitcast_fusion
  133.4 3.1 %fusion.1 = f32[24,8,512]{2,1,0:T(8,128)} fusion(f32[1,8,512]{2,1,0:T(8,128)S(1)} %bitcast.120, f32[24,10,514]{2,1,0:T(8,128)S(1)} %get-tuple-element.28, f32[24,10,514]{2,1,0:T(8,128)S(1)} %get-tuple-element.27, f32[24,8,512]{2,1,0:T(8,128)S(1)} %get-tuple-element.7, f32[24,8,512]{2,1,0:T(8,128)S(1)} %get-tuple-element.14, ...), kind=kLoop, calls=%fused_computation.17 | loop fusion | flops 5996544 | bytes 8273920 | tf_op jit(solution)/shard_map/div | solution.py:88
  (41 shorter events, 0.8 us)
Async XLA Ops:
  0.6 37.3 %copy-start = (f32[24,8,512]{2,1,0:T(8,128)S(1)}, f32[24,8,512]{2,1,0:T(8,128)}, u32[]{:S(2)}) copy-start(f32[24,8,512]{2,1,0:T(8,128)} %param.12) | copy-start | bytes 1179652
  0.6 37.2 %copy-start.7 = (f32[32,128]{1,0:T(8,128)S(1)}, f32[32,128]{1,0:T(8,128)}, u32[]{:S(2)}) copy-start(f32[32,128]{1,0:T(8,128)} %param.18) | copy-start | bytes 49156
  0.7 37.2 %copy-start.8 = (f32[32,128]{1,0:T(8,128)S(1)}, f32[32,128]{1,0:T(8,128)}, u32[]{:S(2)}) copy-start(f32[32,128]{1,0:T(8,128)} %param.19) | copy-start | bytes 49156
  0.7 37.2 %copy-start.4 = (f32[32,128]{1,0:T(8,128)S(1)}, f32[32,128]{1,0:T(8,128)}, u32[]{:S(2)}) copy-start(f32[32,128]{1,0:T(8,128)} %param.20) | copy-start | bytes 49156
  0.7 37.2 %copy-start.5 = (s32[32,128]{1,0:T(8,128)S(1)}, s32[32,128]{1,0:T(8,128)}, u32[]{:S(2)}) copy-start(s32[32,128]{1,0:T(8,128)} %param.23) | copy-start | bytes 49156
  5.6 40.0 %copy-start.6 = (s32[32,128]{1,0:T(8,128)S(1)}, s32[32,128]{1,0:T(8,128)}, u32[]{:S(2)}) copy-start(s32[32,128]{1,0:T(8,128)} %param.22) | copy-start | bytes 49156
  5.6 44.4 %copy-start.9 = (f32[32,128]{1,0:T(8,128)S(1)}, f32[32,128]{1,0:T(8,128)}, u32[]{:S(2)}) copy-start(f32[32,128]{1,0:T(8,128)} %param.21) | copy-start | bytes 49156
  5.6 63.5 %copy-start.3 = (f32[12]{0:T(128)S(1)}, f32[12]{0:T(128)}, u32[]{:S(2)}) copy-start(f32[12]{0:T(128)} %param.14) | copy-start | bytes 148
  32.5 9.9 %all-to-all-start = ((f32[8,4,128]{2,0,1:T(8,128)}), f32[8,4,128]{2,0,1:T(8,128)S(1)}, u32[]{:S(2)}, u32[]{:S(2)}) async-start(f32[8,4,128]{2,0,1:T(8,128)} %slice_bitcast_fusion.10), calls=%async_computation | async-start | bytes 32768 | tf_op jit(solution)/shard_map/all_to_all | solution.py:160
  42.3 7.7 %all-to-all-start.1 = ((f32[8,4,128]{2,0,1:T(8,128)}), f32[8,4,128]{2,0,1:T(8,128)S(1)}, u32[]{:S(2)}, u32[]{:S(2)}) async-start(f32[8,4,128]{2,0,1:T(8,128)} %slice_bitcast_fusion.11), calls=%async_computation.1 | async-start | bytes 32768 | tf_op jit(solution)/shard_map/all_to_all | solution.py:159
  50.1 13.6 %collective-permute-start.5 = (f32[6,3,128]{2,1,0:T(4,128)S(1)}, f32[6,3,128]{2,1,0:T(4,128)S(1)}, u32[]{:S(2)}, u32[]{:S(2)}) collective-permute-start(f32[6,3,128]{2,1,0:T(4,128)S(1)} %get-tuple-element.50), channel_id=1, source_target_pairs={{8,0},{16,8},{24,16},{9,1},{17,9},{25,17},{10,2},{18,10},{26,18},{... | collective-permute-start | bytes 27656 | tf_op jit(solution)/shard_map/ppermute | solution.py:27
  55.2 8.5 %collective-permute-start.4 = (f32[6,3,128]{2,1,0:T(4,128)S(1)}, f32[6,3,128]{2,1,0:T(4,128)S(1)}, u32[]{:S(2)}, u32[]{:S(2)}) collective-permute-start(f32[6,3,128]{2,1,0:T(4,128)S(1)} %get-tuple-element.49), channel_id=1, source_target_pairs={{0,8},{8,16},{16,24},{1,9},{9,17},{17,25},{2,10},{10,18},{18,26},{... | collective-permute-start | bytes 27656 | tf_op jit(solution)/shard_map/ppermute | solution.py:26
  58.4 15.0 %collective-permute-start.1 = (f32[2,24,1,512]{3,2,1,0:T(1,128)S(1)}, f32[2,24,1,512]{3,2,1,0:T(1,128)S(1)}, u32[]{:S(2)}, u32[]{:S(2)}) collective-permute-start(f32[2,24,1,512]{3,2,1,0:T(1,128)S(1)} %get-tuple-element.38), channel_id=1, source_target_pairs={{1,0},{2,1},{3,2},{8,3},{9,8},{10,9},{11,10},{16,11},{17,16},{18,1... | collective-permute-start | bytes 294920 | tf_op jit(solution)/shard_map/ppermute | solution.py:27
  60.3 13.1 %collective-permute-start = (f32[2,24,1,512]{3,2,1,0:T(1,128)S(1)}, f32[2,24,1,512]{3,2,1,0:T(1,128)S(1)}, u32[]{:S(2)}, u32[]{:S(2)}) collective-permute-start(f32[2,24,1,512]{3,2,1,0:T(1,128)S(1)} %get-tuple-element.37), channel_id=1, source_target_pairs={{0,1},{1,2},{2,3},{3,8},{8,9},{9,10},{10,11},{11,16},{16,17},{17,1... | collective-permute-start | bytes 294920 | tf_op jit(solution)/shard_map/ppermute | solution.py:26
  63.8 8.2 %collective-permute-start.7 = (f32[6,38,3]{2,1,0:T(8,128)S(1)}, f32[6,38,3]{2,1,0:T(8,128)S(1)}, u32[]{:S(2)}, u32[]{:S(2)}) collective-permute-start(f32[6,38,3]{2,1,0:T(8,128)S(1)} %get-tuple-element.48), channel_id=1, source_target_pairs={{1,0},{2,1},{3,2},{4,3},{5,4},{6,5},{7,6},{9,8},{10,9},{11,10},{12... | collective-permute-start | bytes 8216 | tf_op jit(solution)/shard_map/ppermute | solution.py:27
  65.1 6.9 %collective-permute-start.6 = (f32[6,38,3]{2,1,0:T(8,128)S(1)}, f32[6,38,3]{2,1,0:T(8,128)S(1)}, u32[]{:S(2)}, u32[]{:S(2)}) collective-permute-start(f32[6,38,3]{2,1,0:T(8,128)S(1)} %get-tuple-element.47), channel_id=1, source_target_pairs={{0,1},{1,2},{2,3},{3,4},{4,5},{5,6},{6,7},{8,9},{9,10},{10,11},{11... | collective-permute-start | bytes 8216 | tf_op jit(solution)/shard_map/ppermute | solution.py:26
  73.4 0.6 copy-start.1
  73.4 0.7 copy-start.2
  74.1 17.9 %collective-permute-start.3 = (f32[2,24,10,1]{3,2,1,0:T(8,128)S(1)}, f32[2,24,10,1]{3,2,1,0:T(8,128)S(1)}, u32[]{:S(2)}, u32[]{:S(2)}) collective-permute-start(f32[2,24,10,1]{3,2,1,0:T(8,128)S(1)} %get-tuple-element.34), channel_id=1, source_target_pairs={{4,0},{5,1},{6,2},{7,3},{12,8},{13,9},{14,10},{15,11},{20,16},{21,... | collective-permute-start | bytes 5768 | tf_op jit(solution)/shard_map/ppermute | solution.py:27
  75.4 17.6 %collective-permute-start.2 = (f32[2,24,10,1]{3,2,1,0:T(8,128)S(1)}, f32[2,24,10,1]{3,2,1,0:T(8,128)S(1)}, u32[]{:S(2)}, u32[]{:S(2)}) collective-permute-start(f32[2,24,10,1]{3,2,1,0:T(8,128)S(1)} %get-tuple-element.33), channel_id=1, source_target_pairs={{0,4},{1,5},{2,6},{3,7},{8,12},{9,13},{10,14},{11,15},{16,20},{17,... | collective-permute-start | bytes 5768 | tf_op jit(solution)/shard_map/ppermute | solution.py:26
  85.5 9.9 %all-to-all-start.2 = ((f32[4,8,128]{2,1,0:T(8,128)}), f32[4,8,128]{2,1,0:T(8,128)S(1)}, u32[]{:S(2)}, u32[]{:S(2)}) async-start(f32[4,8,128]{2,1,0:T(8,128)} %get-tuple-element.46), calls=%async_computation.2 | async-start | bytes 32768 | tf_op jit(solution)/shard_map/all_to_all | solution.py:181
  107.4 5.4 %collective-permute-start.9 = (f32[2,24,1,512]{3,2,1,0:T(1,128)S(1)}, f32[2,24,1,512]{3,2,1,0:T(1,128)S(1)}, u32[]{:S(2)}, u32[]{:S(2)}) collective-permute-start(f32[2,24,1,512]{3,2,1,0:T(1,128)S(1)} %get-tuple-element.36), channel_id=1, source_target_pairs={{1,0},{2,1},{3,2},{8,3},{9,8},{10,9},{11,10},{16,11},{17,16},{18,1... | collective-permute-start | bytes 294920 | tf_op jit(solution)/shard_map/ppermute | solution.py:27
  110.8 8.3 %collective-permute-start.8 = (f32[2,24,1,512]{3,2,1,0:T(1,128)S(1)}, f32[2,24,1,512]{3,2,1,0:T(1,128)S(1)}, u32[]{:S(2)}, u32[]{:S(2)}) collective-permute-start(f32[2,24,1,512]{3,2,1,0:T(1,128)S(1)} %get-tuple-element.35), channel_id=1, source_target_pairs={{0,1},{1,2},{2,3},{3,8},{8,9},{9,10},{10,11},{11,16},{16,17},{17,1... | collective-permute-start | bytes 294920 | tf_op jit(solution)/shard_map/ppermute | solution.py:26
  119.4 10.7 %collective-permute-start.11 = (f32[2,24,10,1]{3,2,1,0:T(8,128)S(1)}, f32[2,24,10,1]{3,2,1,0:T(8,128)S(1)}, u32[]{:S(2)}, u32[]{:S(2)}) collective-permute-start(f32[2,24,10,1]{3,2,1,0:T(8,128)S(1)} %get-tuple-element.32), channel_id=1, source_target_pairs={{4,0},{5,1},{6,2},{7,3},{12,8},{13,9},{14,10},{15,11},{20,16},{21,... | collective-permute-start | bytes 5768 | tf_op jit(solution)/shard_map/ppermute | solution.py:27
  120.7 11.1 %collective-permute-start.10 = (f32[2,24,10,1]{3,2,1,0:T(8,128)S(1)}, f32[2,24,10,1]{3,2,1,0:T(8,128)S(1)}, u32[]{:S(2)}, u32[]{:S(2)}) collective-permute-start(f32[2,24,10,1]{3,2,1,0:T(8,128)S(1)} %get-tuple-element.31), channel_id=1, source_target_pairs={{0,4},{1,5},{2,6},{3,7},{8,12},{9,13},{10,14},{11,15},{16,20},{17,... | collective-permute-start | bytes 5768 | tf_op jit(solution)/shard_map/ppermute | solution.py:26
where the time goes:
time: 138 us; the launch traced here: 136 us
  starting transfers between devices  52.4 us (38%)
  other arithmetic  48.3 us (35%)
  waiting for transfers between devices  27.7 us (20%)
  local copies, waits for them, and re-layouts  6.96 us (5%)
    mul x1, other arithmetic, closures(): conductivity * jnp.sqrt(saturation)  26.2 us
    ppermute x6, starting transfers between devices, with_halo(): before = lax.ppermute(last, axis, up)  26.1 us
    ppermute x6, starting transfers between devices, with_halo(): after = lax.ppermute(leading, axis, down)  14.4 us
    another operation x1, other arithmetic, local(): jnp.stack([head, conduct])  11.8 us
    ppermute x6, waiting for transfers between devices, with_halo(): after = lax.ppermute(leading, axis, down)  10.4 us
    ppermute x6, waiting for transfers between devices, with_halo(): before = lax.ppermute(last, axis, up)  9.1 us
    all_to_all x1, starting transfers between devices, local(): lax.all_to_all(top_conduct, 'gy', split_axis=1, concat_axis=0, tiled=True)  5.41 us
    slice x4, local copies, waits for them, and re-layouts, lookup(): filled = jnp.where(soil_class == kind_number, table[kind_number], filled)  4.97 us
  transfers between devices with their start and end apart: 15, of which 8 were waited for; matrix products, arithmetic and copies ran while one was open for 4% of the time, Pallas kernels for 0%

commit v1 on v0

--- a/solution.py
+++ b/solution.py
@@ -156,7 +156,12 @@
     )
     top_conduct = conduct[0]
     top, top_surface = (
-        lax.all_to_all(pressure[0], "gy", split_axis=1, concat_axis=0, tiled=True),
+        jnp.concatenate(
+            lax.all_to_all(
+                jnp.stack(jnp.split(pressure[0], lax.axis_size("gy"), axis=1)), "gy", 0, 0
+            ),
+            axis=0,
+        ),
         lax.all_to_all(top_conduct, "gy", split_axis=1, concat_axis=0, tiled=True),
     )
     leak = LEAKANCE * land_mask.astype(jnp.float32) * top_surface

time: 138 us -> 138 us (level)
  no operation moved by 1% of the time
where the time goes in v1:
time: 138 us; the launch traced here: 137 us
  starting transfers between devices  52.4 us (38%)
  other arithmetic  49 us (36%)
  waiting for transfers between devices  27.7 us (20%)
  local copies, waits for them, and re-layouts  6.39 us (5%)
    mul x1, other arithmetic, closures(): conductivity * jnp.sqrt(saturation)  26.2 us
    ppermute x6, starting transfers between devices, with_halo(): before = lax.ppermute(last, axis, up)  26.1 us
    ppermute x6, starting transfers between devices, with_halo(): after = lax.ppermute(leading, axis, down)  14.4 us
    another operation x1, other arithmetic, local(): jnp.stack([head, conduct])  11.9 us
    ppermute x6, waiting for transfers between devices, with_halo(): after = lax.ppermute(leading, axis, down)  10.4 us
    ppermute x6, waiting for transfers between devices, with_halo(): before = lax.ppermute(last, axis, up)  9.1 us
    all_to_all x1, starting transfers between devices, local(): lax.all_to_all(top_conduct, 'gy', split_axis=1, concat_axis=0, tiled=True)  5.41 us
    slice x4, local copies, waits for them, and re-layouts, lookup(): filled = jnp.where(soil_class == kind_number, table[kind_number], filled)  4.98 us
  transfers between devices with their start and end apart: 15, of which 8 were waited for; matrix products, arithmetic and copies ran while one was open for 4% of the time, Pallas kernels for 0%

profile of v1, /device:TPU:1, one launch (start us, length us, event | category | flops | bytes accessed | tf_op | source)
XLA Modules:
  0.0 136.6 jit_solution(4487403456805375125)
XLA Ops:
  0.7 1.8 %fusion.114 = (f32[1]{0:T(128)}, f32[1]{0:T(128)}, f32[1]{0:T(128)}, f32[1]{0:T(128)}, f32[1]{0:T(128)}, /*index=5*/f32[1]{0:T(128)}, f32[1]{0:T(128)}, f32[1]{0...) fusion(f32[12]{0:T(128)} %param.15), kind=kLoop, calls=%fused_computation.236 | loop fusion | bytes 96 | tf_op jit(solution)/shard_map/slice | solution.py:37
  2.5 1.8 %fusion.113 = (f32[1]{0:T(128)}, f32[1]{0:T(128)}, f32[1]{0:T(128)}, f32[1]{0:T(128)}, f32[1]{0:T(128)}, /*index=5*/f32[1]{0:T(128)}, f32[1]{0:T(128)}, f32[1]{0...) fusion(f32[12]{0:T(128)} %param.17), kind=kLoop, calls=%fused_computation.235 | loop fusion | bytes 96 | tf_op jit(solution)/shard_map/slice | solution.py:37
  4.3 0.7 divide_subtract_fusion
  4.9 0.7 fusion.112
  5.6 26.2 %multiply_multiply_fusion = (f32[24,8,512]{2,1,0:T(8,128)S(1)}, f32[24,8,512]{2,1,0:T(8,128)S(1)}, f32[24,8,512]{2,1,0:T(8,128)S(1)}, f32[24,8,512]{2,1,0:T(8,12...) fusion(f32[24,8,512]{2,1,0:T(8,128)} %param.12, ...), kind=kLoop, calls=%fused_computation.100 | loop fusion | flops 6094848 | bytes 3539088 | tf_op jit(solution)/shard_map/mul | solution.py:53
  31.9 0.6 slice_bitcast_fusion.10
  32.5 5.4 %all-to-all-start = ((f32[8,4,128]{2,0,1:T(8,128)}), f32[8,4,128]{2,0,1:T(8,128)S(1)}, u32[]{:S(2)}, u32[]{:S(2)}) async-start(f32[8,4,128]{2,0,1:T(8,128)} %slice_bitcast_fusion.10), calls=%async_computation | async-start | bytes 32768 | tf_op jit(solution)/shard_map/all_to_all | solution.py:165
  38.0 0.6 pad_maximum_fusion.16
  38.6 3.8 %all-to-all-done = f32[8,4,128]{2,0,1:T(8,128)S(1)} async-done(((f32[8,4,128]{2,0,1:T(8,128)}), f32[8,4,128]{2,0,1:T(8,128)S(1)}, u32[]{:S(2)}, u32[]{:S(2)}) %all-to-all-start) | async-done | bytes 16416 | tf_op jit(solution)/shard_map/all_to_all | solution.py:165
  42.3 3.2 %all-to-all-start.1 = ((f32[4,8,128]{2,1,0:T(8,128)}), f32[4,8,128]{2,1,0:T(8,128)S(1)}, u32[]{:S(2)}, u32[]{:S(2)}) async-start(f32[4,8,128]{2,1,0:T(8,128)} %pad_maximum_fusion.16), calls=%async_computation.1 | async-start | bytes 32768 | tf_op jit(solution)/shard_map/all_to_all | solution.py:160
  45.6 4.4 %all-to-all-done.1 = f32[4,8,128]{2,1,0:T(8,128)S(1)} async-done(((f32[4,8,128]{2,1,0:T(8,128)}), f32[4,8,128]{2,1,0:T(8,128)S(1)}, u32[]{:S(2)}, u32[]{:S(2)}) %all-to-all-start.1) | async-done | bytes 16416 | tf_op jit(solution)/shard_map/all_to_all | solution.py:160
  50.0 5.2 %collective-permute-start.5 = (f32[6,3,128]{2,1,0:T(4,128)S(1)}, f32[6,3,128]{2,1,0:T(4,128)S(1)}, u32[]{:S(2)}, u32[]{:S(2)}) collective-permute-start(f32[6,3,128]{2,1,0:T(4,128)S(1)} %get-tuple-element.50), channel_id=1, source_target_pairs={{8,0},{16,8},{24,16},{9,1},{17,9},{25,17},{10,2},{18,10},{26,18},{... | collective-permute-start | bytes 27656 | tf_op jit(solution)/shard_map/ppermute | solution.py:27
  55.2 3.0 %collective-permute-start.4 = (f32[6,3,128]{2,1,0:T(4,128)S(1)}, f32[6,3,128]{2,1,0:T(4,128)S(1)}, u32[]{:S(2)}, u32[]{:S(2)}) collective-permute-start(f32[6,3,128]{2,1,0:T(4,128)S(1)} %get-tuple-element.49), channel_id=1, source_target_pairs={{0,8},{8,16},{16,24},{1,9},{9,17},{17,25},{2,10},{10,18},{18,26},{... | collective-permute-start | bytes 27656 | tf_op jit(solution)/shard_map/ppermute | solution.py:26
  58.4 1.9 %collective-permute-start.1 = (f32[2,24,1,512]{3,2,1,0:T(1,128)S(1)}, f32[2,24,1,512]{3,2,1,0:T(1,128)S(1)}, u32[]{:S(2)}, u32[]{:S(2)}) collective-permute-start(f32[2,24,1,512]{3,2,1,0:T(1,128)S(1)} %get-tuple-element.38), channel_id=1, source_target_pairs={{1,0},{2,1},{3,2},{8,3},{9,8},{10,9},{11,10},{16,11},{17,16},{18,1... | collective-permute-start | bytes 294920 | tf_op jit(solution)/shard_map/ppermute | solution.py:27
  60.3 3.4 %collective-permute-start = (f32[2,24,1,512]{3,2,1,0:T(1,128)S(1)}, f32[2,24,1,512]{3,2,1,0:T(1,128)S(1)}, u32[]{:S(2)}, u32[]{:S(2)}) collective-permute-start(f32[2,24,1,512]{3,2,1,0:T(1,128)S(1)} %get-tuple-element.37), channel_id=1, source_target_pairs={{0,1},{1,2},{2,3},{3,8},{8,9},{9,10},{10,11},{11,16},{16,17},{17,1... | collective-permute-start | bytes 294920 | tf_op jit(solution)/shard_map/ppermute | solution.py:26
  63.8 1.3 collective-permute-start.7
  65.1 4.0 %collective-permute-start.6 = (f32[6,38,3]{2,1,0:T(8,128)S(1)}, f32[6,38,3]{2,1,0:T(8,128)S(1)}, u32[]{:S(2)}, u32[]{:S(2)}) collective-permute-start(f32[6,38,3]{2,1,0:T(8,128)S(1)} %get-tuple-element.47), channel_id=1, source_target_pairs={{0,1},{1,2},{2,3},{3,4},{4,5},{5,6},{6,7},{8,9},{9,10},{10,11},{11... | collective-permute-start | bytes 8216 | tf_op jit(solution)/shard_map/ppermute | solution.py:26
  69.1 0.7 fusion.111
  69.8 2.2 %collective-permute-done.7 = f32[6,38,3]{2,1,0:T(8,128)S(1)} collective-permute-done((f32[6,38,3]{2,1,0:T(8,128)S(1)}, f32[6,38,3]{2,1,0:T(8,128)S(1)}, u32[]{:S(2)}, u32[]{:S(2)}) %collective-permute-start.7) | collective-permute-done | bytes 2768 | tf_op jit(solution)/shard_map/ppermute | solution.py:27
  72.0 0.2 pad_maximum_fusion.10
  72.2 0.1 fusion.78
  72.4 0.2 fusion.82
  72.5 0.1 slice_add_fusion.1
  72.7 0.1 fusion.64
  72.8 0.2 fusion.68
  73.0 0.1 slice_add_fusion
  73.4 0.3 pad_maximum_fusion.9
  73.7 0.3 copy-done.1
  74.0 1.3 collective-permute-start.3
  75.3 9.5 %collective-permute-start.2 = (f32[2,24,10,1]{3,2,1,0:T(8,128)S(1)}, f32[2,24,10,1]{3,2,1,0:T(8,128)S(1)}, u32[]{:S(2)}, u32[]{:S(2)}) collective-permute-start(f32[2,24,10,1]{3,2,1,0:T(8,128)S(1)} %get-tuple-element.33), channel_id=1, source_target_pairs={{0,4},{1,5},{2,6},{3,7},{8,12},{9,13},{10,14},{11,15},{16,20},{17,... | collective-permute-start | bytes 5768 | tf_op jit(solution)/shard_map/ppermute | solution.py:26
  84.8 0.7 fusion.96
  85.5 3.2 %all-to-all-start.2 = ((f32[4,8,128]{2,1,0:T(8,128)}), f32[4,8,128]{2,1,0:T(8,128)S(1)}, u32[]{:S(2)}, u32[]{:S(2)}) async-start(f32[4,8,128]{2,1,0:T(8,128)} %get-tuple-element.46), calls=%async_computation.2 | async-start | bytes 32768 | tf_op jit(solution)/shard_map/all_to_all | solution.py:186
  88.8 3.2 %collective-permute-done.3 = f32[2,24,10,1]{3,2,1,0:T(8,128)S(1)} collective-permute-done((f32[2,24,10,1]{3,2,1,0:T(8,128)S(1)}, f32[2,24,10,1]{3,2,1,0:T(8,128)S(1)}, u32[]{:S(2)}, u32[]{:S(2)}) %collective-permute-start.3) | collective-permute-done | bytes 1952 | tf_op jit(solution)/shard_map/ppermute | solution.py:27
  92.0 0.9 collective-permute-done.2
  92.9 2.4 %pad_maximum_fusion = f32[2,24,10,514]{3,2,1,0:T(8,128)S(1)} fusion(f32[2,24,10,1]{3,2,1,0:T(8,128)S(1)} %collective-permute-done.3, f32[2,24,1,512]{3,2,1,0:T(1,128)} %copy-done.1, f32[1,24,8,512]{3,2,1,0:T(8,128)S(1)} %bitcast.124, f32[1,24,8,512]{3,2,1,0:T(8,128)S(1)} %bitcast.118, f32[2,24,1,512]{3,2,1,0:T(1,128)} %copy-done.2, ...), kind=kLoop, calls=%fused_computation | loop fusion | flops 1233600 | bytes 1973760 | tf_op jit(solution)/shard_map/concatenate | solution.py:28
  95.3 0.1 slice_bitcast_fusion.2
  95.4 11.9 %multiply_bitcast_fusion = (f32[1,24,8,512]{3,2,1,0:T(8,128)S(1)}, f32[24,8,512]{2,1,0:T(8,128)S(1)}, f32[24,8,512]{2,1,0:T(8,128)S(1)}) fusion(f32[24,8,512]{2,1,0:T(8,128)S(1)} %get-tuple-element.14, f32[24,8,512]{2,1,0:T(8,128)S(1)} %get-tuple-element.13, f32[24,8,512]{2,1,0:T(8,128)S(1)} %get-tuple-element.12, f32[1,8,512]{2,1,0:T(8,128)S(1)} %bitcast.125, ...), kind=kLoop, calls=%fused_computation.94 | loop fusion | flops 7667712 | bytes 9846832 | tf_op jit(solution)/shard_map/stack | solution.py:190
  107.4 3.4 %collective-permute-start.9 = (f32[2,24,1,512]{3,2,1,0:T(1,128)S(1)}, f32[2,24,1,512]{3,2,1,0:T(1,128)S(1)}, u32[]{:S(2)}, u32[]{:S(2)}) collective-permute-start(f32[2,24,1,512]{3,2,1,0:T(1,128)S(1)} %get-tuple-element.36), channel_id=1, source_target_pairs={{1,0},{2,1},{3,2},{8,3},{9,8},{10,9},{11,10},{16,11},{17,16},{18,1... | collective-permute-start | bytes 294920 | tf_op jit(solution)/shard_map/ppermute | solution.py:27
  110.9 1.9 %collective-permute-start.8 = (f32[2,24,1,512]{3,2,1,0:T(1,128)S(1)}, f32[2,24,1,512]{3,2,1,0:T(1,128)S(1)}, u32[]{:S(2)}, u32[]{:S(2)}) collective-permute-start(f32[2,24,1,512]{3,2,1,0:T(1,128)S(1)} %get-tuple-element.35), channel_id=1, source_target_pairs={{0,1},{1,2},{2,3},{3,8},{8,9},{9,10},{10,11},{11,16},{16,17},{17,1... | collective-permute-start | bytes 294920 | tf_op jit(solution)/shard_map/ppermute | solution.py:26
  112.8 6.4 %collective-permute-done.8 = f32[2,24,1,512]{3,2,1,0:T(1,128)S(1)} collective-permute-done((f32[2,24,1,512]{3,2,1,0:T(1,128)S(1)}, f32[2,24,1,512]{3,2,1,0:T(1,128)S(1)}, u32[]{:S(2)}, u32[]{:S(2)}) %collective-permute-start.8) | collective-permute-done | bytes 98336 | tf_op jit(solution)/shard_map/ppermute | solution.py:26
  119.2 0.3 pad_maximum_fusion.5
  119.5 1.3 collective-permute-start.11
  120.8 4.3 %collective-permute-start.10 = (f32[2,24,10,1]{3,2,1,0:T(8,128)S(1)}, f32[2,24,10,1]{3,2,1,0:T(8,128)S(1)}, u32[]{:S(2)}, u32[]{:S(2)}) collective-permute-start(f32[2,24,10,1]{3,2,1,0:T(8,128)S(1)} %get-tuple-element.31), channel_id=1, source_target_pairs={{0,4},{1,5},{2,6},{3,7},{8,12},{9,13},{10,14},{11,15},{16,20},{17,... | collective-permute-start | bytes 5768 | tf_op jit(solution)/shard_map/ppermute | solution.py:26
  125.1 5.0 %collective-permute-done.11 = f32[2,24,10,1]{3,2,1,0:T(8,128)S(1)} collective-permute-done((f32[2,24,10,1]{3,2,1,0:T(8,128)S(1)}, f32[2,24,10,1]{3,2,1,0:T(8,128)S(1)}, u32[]{:S(2)}, u32[]{:S(2)}) %collective-permute-start.11) | collective-permute-done | bytes 1952 | tf_op jit(solution)/shard_map/ppermute | solution.py:27
  130.1 1.8 %collective-permute-done.10 = f32[2,24,10,1]{3,2,1,0:T(8,128)S(1)} collective-permute-done((f32[2,24,10,1]{3,2,1,0:T(8,128)S(1)}, f32[2,24,10,1]{3,2,1,0:T(8,128)S(1)}, u32[]{:S(2)}, u32[]{:S(2)}) %collective-permute-start.10) | collective-permute-done | bytes 1952 | tf_op jit(solution)/shard_map/ppermute | solution.py:26
  131.9 1.4 %pad_maximum_fusion.1 = f32[2,24,10,514]{3,2,1,0:T(8,128)S(1)} fusion(f32[2,24,10,1]{3,2,1,0:T(8,128)S(1)} %collective-permute-done.11, f32[2,24,1,512]{3,2,1,0:T(1,128)S(1)} %collective-permute-done.9, f32[1,24,8,512]{3,2,1,0:T(8,128)S(1)} %get-tuple-element.5, f32[1,24,8,512]{3,2,1,0:T(8,128)S(1)} %bitcast.121, ...), kind=kLoop, calls=%fused_computation.1 | loop fusion | flops 1233600 | bytes 1973760 | tf_op jit(solution)/shard_map/concatenate | solution.py:28
  133.3 0.1 slice_bitcast_fusion
  133.5 3.1 %fusion.1 = f32[24,8,512]{2,1,0:T(8,128)} fusion(f32[1,8,512]{2,1,0:T(8,128)S(1)} %bitcast.126, f32[24,10,514]{2,1,0:T(8,128)S(1)} %get-tuple-element.28, f32[24,10,514]{2,1,0:T(8,128)S(1)} %get-tuple-element.27, f32[24,8,512]{2,1,0:T(8,128)S(1)} %get-tuple-element.7, f32[24,8,512]{2,1,0:T(8,128)S(1)} %get-tuple-element.14, ...), kind=kLoop, calls=%fused_computation.17 | loop fusion | flops 5996544 | bytes 8273920 | tf_op jit(solution)/shard_map/div | solution.py:88
  (43 shorter events, 0.8 us)
Async XLA Ops:
  0.6 37.2 %copy-start = (f32[24,8,512]{2,1,0:T(8,128)S(1)}, f32[24,8,512]{2,1,0:T(8,128)}, u32[]{:S(2)}) copy-start(f32[24,8,512]{2,1,0:T(8,128)} %param.12) | copy-start | bytes 1179652
  0.6 37.2 %copy-start.7 = (f32[32,128]{1,0:T(8,128)S(1)}, f32[32,128]{1,0:T(8,128)}, u32[]{:S(2)}) copy-start(f32[32,128]{1,0:T(8,128)} %param.18) | copy-start | bytes 49156
  0.7 37.3 %copy-start.8 = (f32[32,128]{1,0:T(8,128)S(1)}, f32[32,128]{1,0:T(8,128)}, u32[]{:S(2)}) copy-start(f32[32,128]{1,0:T(8,128)} %param.19) | copy-start | bytes 49156
  0.7 37.3 %copy-start.4 = (f32[32,128]{1,0:T(8,128)S(1)}, f32[32,128]{1,0:T(8,128)}, u32[]{:S(2)}) copy-start(f32[32,128]{1,0:T(8,128)} %param.20) | copy-start | bytes 49156
  0.7 37.3 %copy-start.5 = (s32[32,128]{1,0:T(8,128)S(1)}, s32[32,128]{1,0:T(8,128)}, u32[]{:S(2)}) copy-start(s32[32,128]{1,0:T(8,128)} %param.23) | copy-start | bytes 49156
  5.6 39.9 %copy-start.6 = (s32[32,128]{1,0:T(8,128)S(1)}, s32[32,128]{1,0:T(8,128)}, u32[]{:S(2)}) copy-start(s32[32,128]{1,0:T(8,128)} %param.22) | copy-start | bytes 49156
  5.6 44.4 %copy-start.9 = (f32[32,128]{1,0:T(8,128)S(1)}, f32[32,128]{1,0:T(8,128)}, u32[]{:S(2)}) copy-start(f32[32,128]{1,0:T(8,128)} %param.21) | copy-start | bytes 49156
  31.8 37.3 %copy-start.3 = (f32[12]{0:T(128)S(1)}, f32[12]{0:T(128)}, u32[]{:S(2)}) copy-start(f32[12]{0:T(128)} %param.14) | copy-start | bytes 148
  32.5 9.9 %all-to-all-start = ((f32[8,4,128]{2,0,1:T(8,128)}), f32[8,4,128]{2,0,1:T(8,128)S(1)}, u32[]{:S(2)}, u32[]{:S(2)}) async-start(f32[8,4,128]{2,0,1:T(8,128)} %slice_bitcast_fusion.10), calls=%async_computation | async-start | bytes 32768 | tf_op jit(solution)/shard_map/all_to_all | solution.py:165
  42.3 7.7 %all-to-all-start.1 = ((f32[4,8,128]{2,1,0:T(8,128)}), f32[4,8,128]{2,1,0:T(8,128)S(1)}, u32[]{:S(2)}, u32[]{:S(2)}) async-start(f32[4,8,128]{2,1,0:T(8,128)} %pad_maximum_fusion.16), calls=%async_computation.1 | async-start | bytes 32768 | tf_op jit(solution)/shard_map/all_to_all | solution.py:160
  50.0 13.6 %collective-permute-start.5 = (f32[6,3,128]{2,1,0:T(4,128)S(1)}, f32[6,3,128]{2,1,0:T(4,128)S(1)}, u32[]{:S(2)}, u32[]{:S(2)}) collective-permute-start(f32[6,3,128]{2,1,0:T(4,128)S(1)} %get-tuple-element.50), channel_id=1, source_target_pairs={{8,0},{16,8},{24,16},{9,1},{17,9},{25,17},{10,2},{18,10},{26,18},{... | collective-permute-start | bytes 27656 | tf_op jit(solution)/shard_map/ppermute | solution.py:27
  55.2 8.5 %collective-permute-start.4 = (f32[6,3,128]{2,1,0:T(4,128)S(1)}, f32[6,3,128]{2,1,0:T(4,128)S(1)}, u32[]{:S(2)}, u32[]{:S(2)}) collective-permute-start(f32[6,3,128]{2,1,0:T(4,128)S(1)} %get-tuple-element.49), channel_id=1, source_target_pairs={{0,8},{8,16},{16,24},{1,9},{9,17},{17,25},{2,10},{10,18},{18,26},{... | collective-permute-start | bytes 27656 | tf_op jit(solution)/shard_map/ppermute | solution.py:26
  58.4 15.0 %collective-permute-start.1 = (f32[2,24,1,512]{3,2,1,0:T(1,128)S(1)}, f32[2,24,1,512]{3,2,1,0:T(1,128)S(1)}, u32[]{:S(2)}, u32[]{:S(2)}) collective-permute-start(f32[2,24,1,512]{3,2,1,0:T(1,128)S(1)} %get-tuple-element.38), channel_id=1, source_target_pairs={{1,0},{2,1},{3,2},{8,3},{9,8},{10,9},{11,10},{16,11},{17,16},{18,1... | collective-permute-start | bytes 294920 | tf_op jit(solution)/shard_map/ppermute | solution.py:27
  60.3 13.1 %collective-permute-start = (f32[2,24,1,512]{3,2,1,0:T(1,128)S(1)}, f32[2,24,1,512]{3,2,1,0:T(1,128)S(1)}, u32[]{:S(2)}, u32[]{:S(2)}) collective-permute-start(f32[2,24,1,512]{3,2,1,0:T(1,128)S(1)} %get-tuple-element.37), channel_id=1, source_target_pairs={{0,1},{1,2},{2,3},{3,8},{8,9},{9,10},{10,11},{11,16},{16,17},{17,1... | collective-permute-start | bytes 294920 | tf_op jit(solution)/shard_map/ppermute | solution.py:26
  63.8 8.2 %collective-permute-start.7 = (f32[6,38,3]{2,1,0:T(8,128)S(1)}, f32[6,38,3]{2,1,0:T(8,128)S(1)}, u32[]{:S(2)}, u32[]{:S(2)}) collective-permute-start(f32[6,38,3]{2,1,0:T(8,128)S(1)} %get-tuple-element.48), channel_id=1, source_target_pairs={{1,0},{2,1},{3,2},{4,3},{5,4},{6,5},{7,6},{9,8},{10,9},{11,10},{12... | collective-permute-start | bytes 8216 | tf_op jit(solution)/shard_map/ppermute | solution.py:27
  65.1 6.9 %collective-permute-start.6 = (f32[6,38,3]{2,1,0:T(8,128)S(1)}, f32[6,38,3]{2,1,0:T(8,128)S(1)}, u32[]{:S(2)}, u32[]{:S(2)}) collective-permute-start(f32[6,38,3]{2,1,0:T(8,128)S(1)} %get-tuple-element.47), channel_id=1, source_target_pairs={{0,1},{1,2},{2,3},{3,4},{4,5},{5,6},{6,7},{8,9},{9,10},{10,11},{11... | collective-permute-start | bytes 8216 | tf_op jit(solution)/shard_map/ppermute | solution.py:26
  73.4 0.6 copy-start.1
  73.4 0.7 copy-start.2
  74.0 17.9 %collective-permute-start.3 = (f32[2,24,10,1]{3,2,1,0:T(8,128)S(1)}, f32[2,24,10,1]{3,2,1,0:T(8,128)S(1)}, u32[]{:S(2)}, u32[]{:S(2)}) collective-permute-start(f32[2,24,10,1]{3,2,1,0:T(8,128)S(1)} %get-tuple-element.34), channel_id=1, source_target_pairs={{4,0},{5,1},{6,2},{7,3},{12,8},{13,9},{14,10},{15,11},{20,16},{21,... | collective-permute-start | bytes 5768 | tf_op jit(solution)/shard_map/ppermute | solution.py:27
  75.3 17.6 %collective-permute-start.2 = (f32[2,24,10,1]{3,2,1,0:T(8,128)S(1)}, f32[2,24,10,1]{3,2,1,0:T(8,128)S(1)}, u32[]{:S(2)}, u32[]{:S(2)}) collective-permute-start(f32[2,24,10,1]{3,2,1,0:T(8,128)S(1)} %get-tuple-element.33), channel_id=1, source_target_pairs={{0,4},{1,5},{2,6},{3,7},{8,12},{9,13},{10,14},{11,15},{16,20},{17,... | collective-permute-start | bytes 5768 | tf_op jit(solution)/shard_map/ppermute | solution.py:26
  85.5 9.9 %all-to-all-start.2 = ((f32[4,8,128]{2,1,0:T(8,128)}), f32[4,8,128]{2,1,0:T(8,128)S(1)}, u32[]{:S(2)}, u32[]{:S(2)}) async-start(f32[4,8,128]{2,1,0:T(8,128)} %get-tuple-element.46), calls=%async_computation.2 | async-start | bytes 32768 | tf_op jit(solution)/shard_map/all_to_all | solution.py:186
  107.4 5.4 %collective-permute-start.9 = (f32[2,24,1,512]{3,2,1,0:T(1,128)S(1)}, f32[2,24,1,512]{3,2,1,0:T(1,128)S(1)}, u32[]{:S(2)}, u32[]{:S(2)}) collective-permute-start(f32[2,24,1,512]{3,2,1,0:T(1,128)S(1)} %get-tuple-element.36), channel_id=1, source_target_pairs={{1,0},{2,1},{3,2},{8,3},{9,8},{10,9},{11,10},{16,11},{17,16},{18,1... | collective-permute-start | bytes 294920 | tf_op jit(solution)/shard_map/ppermute | solution.py:27
  110.9 8.3 %collective-permute-start.8 = (f32[2,24,1,512]{3,2,1,0:T(1,128)S(1)}, f32[2,24,1,512]{3,2,1,0:T(1,128)S(1)}, u32[]{:S(2)}, u32[]{:S(2)}) collective-permute-start(f32[2,24,1,512]{3,2,1,0:T(1,128)S(1)} %get-tuple-element.35), channel_id=1, source_target_pairs={{0,1},{1,2},{2,3},{3,8},{8,9},{9,10},{10,11},{11,16},{16,17},{17,1... | collective-permute-start | bytes 294920 | tf_op jit(solution)/shard_map/ppermute | solution.py:26
  119.5 10.7 %collective-permute-start.11 = (f32[2,24,10,1]{3,2,1,0:T(8,128)S(1)}, f32[2,24,10,1]{3,2,1,0:T(8,128)S(1)}, u32[]{:S(2)}, u32[]{:S(2)}) collective-permute-start(f32[2,24,10,1]{3,2,1,0:T(8,128)S(1)} %get-tuple-element.32), channel_id=1, source_target_pairs={{4,0},{5,1},{6,2},{7,3},{12,8},{13,9},{14,10},{15,11},{20,16},{21,... | collective-permute-start | bytes 5768 | tf_op jit(solution)/shard_map/ppermute | solution.py:27
  120.8 11.1 %collective-permute-start.10 = (f32[2,24,10,1]{3,2,1,0:T(8,128)S(1)}, f32[2,24,10,1]{3,2,1,0:T(8,128)S(1)}, u32[]{:S(2)}, u32[]{:S(2)}) collective-permute-start(f32[2,24,10,1]{3,2,1,0:T(8,128)S(1)} %get-tuple-element.31), channel_id=1, source_target_pairs={{0,4},{1,5},{2,6},{3,7},{8,12},{9,13},{10,14},{11,15},{16,20},{17,... | collective-permute-start | bytes 5768 | tf_op jit(solution)/shard_map/ppermute | solution.py:26
